TPU v7x, 32 devices: a whole 2x2x4 slice. The times are simulated.
32 devices in a mesh: task: 2 (over x), batch: 16 (over z, y, core).
Axes of the slice: x: 2, y: 2, z: 4, core: 2. Of those that a mesh axis runs over, the one named last changes fastest.
Arguments:
- pooled: bfloat16 [12288, 3328], P('batch'), may hold values from -6 to 6
- gate_weight: bfloat16 [3328, 8, 4], P(None, 'task'), may hold values from -0.21875 to 0.21875
- w_first: bfloat16 [8, 3328, 1024], P('task', 'batch'), may hold values from -0.15625 to 0.15625
- w_second: bfloat16 [8, 1024, 512], P('task', 'batch'), may hold values from -0.25 to 0.25
- w_third: bfloat16 [8, 512, 256], P('task', 'batch'), may hold values from -0.375 to 0.375
- tower_hidden: bfloat16 [4, 256, 128], P('task'), may hold values from -0.5 to 0.5
- tower_out: bfloat16 [4, 128], P('task'), may hold values from -0.75 to 0.75
Outputs:
- task_logits: float32 [12288, 4], P('batch', 'task')
All inputs are finite; a program needn't handle non-finite values.
Results may differ from a plain program's by a relative error of at most 0.02.
Values may be sent and summed in bfloat16 or wider, within the bound.
A program may use at most 128 MiB of HBM per device.

v0:
```python
import jax
import jax.numpy as jnp
from jax import lax
from jax.sharding import PartitionSpec as P


def per_device(pooled, gate_weight, w_first, w_second, w_third, tower_hidden, tower_out):
    tok_rows = pooled.shape[0]
    width_in = pooled.shape[1]
    local_experts = w_first.shape[0]
    all_tasks = gate_weight.shape[2]
    own_tasks = tower_hidden.shape[0]
    gathered = lax.all_gather(w_first, "batch", axis=1, tiled=True)
    deep_rows, deep_width = (w_second.shape[1], w_second.shape[2])
    last_rows, last_width = (w_third.shape[1], w_third.shape[2])
    halves = deep_width // last_width
    packed = jnp.concatenate(
        [w_second[:, :, i * last_width : (i + 1) * last_width] for i in range(halves)] + [w_third],
        axis=1,
    )
    gathered, packed = lax.optimization_barrier((gathered, packed))
    packed = lax.all_gather(packed, "batch", axis=1, tiled=False)
    second_all = jnp.concatenate(
        [packed[:, :, i * deep_rows : (i + 1) * deep_rows] for i in range(halves)], axis=3
    ).reshape(local_experts, -1, deep_width)
    third_all = packed[:, :, halves * deep_rows :].reshape(local_experts, -1, last_width)
    summed = jnp.einsum("tr,erh->eth", pooled, gathered, preferred_element_type=jnp.float32)
    first = jax.nn.relu(summed).astype(jnp.bfloat16)
    logits = jnp.dot(
        pooled,
        gate_weight.reshape(width_in, local_experts * all_tasks),
        preferred_element_type=jnp.float32,
    )
    weights = jnp.exp(logits.reshape(tok_rows, local_experts, all_tasks))
    gate_total = jnp.sum(weights, axis=1)
    columns = first
    second = jax.nn.relu(
        jnp.einsum("etr,erh->eth", columns, second_all, preferred_element_type=jnp.float32)
    ).astype(jnp.bfloat16)
    columns = second
    expert_out = jax.nn.relu(
        jnp.einsum("etr,erh->eth", columns, third_all, preferred_element_type=jnp.float32)
    ).astype(jnp.bfloat16)
    numer = jnp.einsum("tek,eth->tkh", weights, expert_out.astype(jnp.float32))
    groups = all_tasks // own_tasks
    me = lax.axis_index("task")
    numer_own = lax.dynamic_slice_in_dim(numer, me * own_tasks, own_tasks, 1)
    total_own = lax.dynamic_slice_in_dim(gate_total, me * own_tasks, own_tasks, 1)
    for shift in range(1, groups):
        ring = [(i, (i + shift) % groups) for i in range(groups)]
        other = lax.rem(me + shift, groups) * own_tasks
        numer_sent = lax.dynamic_slice_in_dim(numer, other, own_tasks, 1).astype(jnp.bfloat16)
        total_sent = lax.dynamic_slice_in_dim(gate_total, other, own_tasks, 1)
        numer_own = numer_own + lax.ppermute(numer_sent, "task", ring).astype(jnp.float32)
        total_own = total_own + lax.ppermute(total_sent, "task", ring)
    mix = (numer_own / total_own[:, :, None]).astype(jnp.bfloat16)
    tower = jax.nn.relu(
        jnp.einsum("tkh,khm->tkm", mix, tower_hidden, preferred_element_type=jnp.float32)
    ).astype(jnp.bfloat16)
    return jnp.einsum("tkm,km->tk", tower, tower_out, preferred_element_type=jnp.float32)


def solution(mesh):
    placed = (
        P("batch", None),
        P(None, "task", None),
        P("task", "batch", None),
        P("task", "batch", None),
        P("task", "batch", None),
        P("task", None, None),
        P("task", None),
    )
    return jax.shard_map(
        per_device, mesh=mesh, in_specs=placed, out_specs=P("batch", "task"), check_vma=False
    )
```

profile of v0, /device:TPU:0, one launch (start us, length us, event | category | flops | bytes accessed | tf_op | source)
XLA Modules:
  0.0 290.8 jit_solution(5870801982256246528)
XLA Ops:
  6.5 0.7 all-gather.4.cloned.1.call-update
  7.3 0.0 all-gather.6.cloned.1.call-start
  7.3 1.0 fusion.32
  8.3 1.6 pad_maximum_fusion.1
  9.9 140.2 %all-gather.4.cloned.1.call-done = bf16[4,3328,1024]{2,1,0:T(8,128)(2,1)} async-done(((bf16[4,208,1024]{2,1,0:T(8,128)(2,1)}), bf16[4,3328,1024]{2,1,0:T(8,128)(2,1)}) %all-gather.4.cloned.1.call-update) | async-done | bytes 27262992 | tf_op jit(solution)/shard_map/all_gather | solution.py:13
  150.1 0.0 all-gather.6.cloned.1.call-update
  150.1 0.9 reshape.12
  151.0 4.1 %fusion.33 = (f32[768,4]{0,1:T(4,128)S(1)}, bf16[768,4,4]{0,2,1:T(4,128)(2,1)S(1)}) fusion(bf16[4,4,3328]{2,1,0:T(4,128)(2,1)S(1)} %dot_general.26, bf16[768,3328]{1,0:T(8,128)(2,1)} %param.7), kind=kOutput, calls=%fused_computation.36 | convolution fusion | flops 81810432 | bytes 5255168 | tf_op jit(solution)/shard_map/dot_general | solution.py:29
  155.1 1.3 copy.9
  156.4 51.7 %all-gather.6.cloned.1.call-done = bf16[4,2560,256]{2,1,0:T(8,128)(2,1)} async-done(((bf16[4,160,256]{2,1,0:T(8,128)(2,1)}), bf16[4,2560,256]{2,1,0:T(8,128)(2,1)}) %all-gather.6.cloned.1.call-update) | async-done | bytes 5242896 | tf_op jit(solution)/shard_map/all_gather | solution.py:22
  208.1 1.3 slice.22
  209.4 2.8 fusion.31
  212.2 2.5 pad_maximum_fusion
  214.7 36.6 %fusion = bf16[4,768,512]{2,1,0:T(8,128)(2,1)} fusion(bf16[4,1024,512]{2,1,0:T(8,128)(2,1)} %bitcast.37, bf16[4,3328,1024]{2,1,0:T(8,128)(2,1)} %all-gather.4.cloned.1.call-done, bf16[768,3328]{1,0:T(8,128)(2,1)} %param.7), kind=kOutput, calls=%fused_computation.1 | convolution fusion | flops 24165482496 | bytes 39714816 | tf_op jit(solution)/shard_map/etr,erh->eth/dot_general | solution.py:38
  251.3 2.9 %fusion.10 = bf16[4,768,256]{2,1,0:T(8,128)(2,1)S(1)} fusion(bf16[4,512,256]{2,1,0:T(8,128)(2,1)S(1)} %bitcast.38, bf16[4,768,512]{2,1,0:T(8,128)(2,1)} %fusion), kind=kOutput, calls=%fused_computation.9 | convolution fusion | flops 810024960 | bytes 5767168 | tf_op jit(solution)/shard_map/etr,erh->eth/dot_general | solution.py:42
  254.2 1.5 fusion.13
  255.8 1.6 dynamic-slice_convert_fusion
  257.4 1.5 collective-permute-start
  258.9 0.6 collective-permute-start.1
  259.4 18.0 %collective-permute-done.1 = f32[768,2]{0,1:T(2,128)S(1)} collective-permute-done((f32[768,2]{0,1:T(2,128)S(1)}, f32[768,2]{0,1:T(2,128)S(1)}, u32[]{:S(2)}, u32[]{:S(2)}) %collective-permute-start.1) | collective-permute-done | bytes 6176 | tf_op jit(solution)/shard_map/ppermute | solution.py:55
  277.5 0.9 copy.10
  278.4 3.2 %fusion.16 = bf16[768,2,256]{2,1,0:T(2,128)(2,1)} fusion(bf16[768,2,256]{2,1,0:T(2,128)(2,1)} %collective-permute-done, f32[768,4,256]{2,1,0:T(4,128)S(1)} %fusion.13, s32[]{:T(128)S(6)} %select_n.8, f32[768,2]{1,0:T(8,128)} %copy.10), kind=kLoop, calls=%fused_computation.17 | loop fusion | flops 1572864 | bytes 3151876 | tf_op jit(solution)/shard_map/convert_element_type | solution.py:56
  281.7 1.6 fusion.19
  283.3 0.6 copy.25
  (11 shorter events, 0.1 us)
Async XLA Ops:
  6.5 275.1 %copy-start = (bf16[2,256,128]{2,1,0:T(8,128)(2,1)S(1)}, bf16[2,256,128]{2,1,0:T(8,128)(2,1)}, u32[]{:S(2)}) copy-start(bf16[2,256,128]{2,1,0:T(8,128)(2,1)} %param.12) | copy-start | bytes 393220
  6.5 143.5 %all-gather.4.cloned.1.call-start = ((), (), s32[]{:S(2)}) async-start(), calls=%async_computation | async-start | bytes 28966912 | tf_op jit(solution)/shard_map/all_gather | solution.py:13
  7.3 200.9 %all-gather.6.cloned.1.call-start = ((), (), s32[]{:S(2)}) async-start(), calls=%async_computation.1 | async-start | bytes 5570560 | tf_op jit(solution)/shard_map/all_gather | solution.py:22
  251.3 3.0 %copy-start.1 = (bf16[768,4,4]{1,2,0:T(4,128)(2,1)S(1)}, bf16[768,4,4]{1,2,0:T(4,128)(2,1)}, u32[]{:S(2)}) copy-start(bf16[768,4,4]{1,2,0:T(4,128)(2,1)} %copy.9) | copy-start | bytes 73732
  255.8 25.9 %copy-start.2 = (bf16[2,128]{1,0:T(2,128)(2,1)S(1)}, bf16[2,128]{1,0:T(2,128)(2,1)}, u32[]{:S(2)}) copy-start(bf16[2,128]{1,0:T(2,128)(2,1)} %param.13) | copy-start | bytes 1540
  257.4 21.0 %collective-permute-start = (bf16[768,2,256]{2,1,0:T(2,128)(2,1)}, bf16[768,2,256]{2,1,0:T(2,128)(2,1)}, u32[]{:S(2)}, u32[]{:S(2)}) collective-permute-start(bf16[768,2,256]{2,1,0:T(2,128)(2,1)} %dynamic-slice_convert_fusion), channel_id=1, source_target_pairs={{0,16},{16,0},{1,17},{17,1},{2,18},{18,2},{3,19},{19,3},{4,20},{20... | collective-permute-start | bytes 2359304 | tf_op jit(solution)/shard_map/ppermute | solution.py:54
  258.9 18.6 %collective-permute-start.1 = (f32[768,2]{0,1:T(2,128)S(1)}, f32[768,2]{0,1:T(2,128)S(1)}, u32[]{:S(2)}, u32[]{:S(2)}) collective-permute-start(f32[768,2]{0,1:T(2,128)S(1)} %constant_dynamic-slice_fusion), channel_id=1, source_target_pairs={{0,16},{16,0},{1,17},{17,1},{2,18},{18,2},{3,19},{19,3},{4,20},{20... | collective-permute-start | bytes 18440 | tf_op jit(solution)/shard_map/ppermute | solution.py:55
Sparse Core Ops, SparseCore 0:
  8.9 141.1 all-gather.3
  152.3 55.7 all-gather.5
where the time goes:
time: 291 us
  waiting for transfers between devices  211 us (73%)
  matrix products  46.7 us (16%)
  between operations  13.5 us (5%)
  local copies, waits for them, and re-layouts  10.6 us (4%)
  other arithmetic  7.28 us (3%)
    all_gather x1, waiting for transfers between devices, per_device(): gathered = lax.all_gather(w_first, 'batch', axis=1, tiled=True)  140 us
    all_gather x1, waiting for transfers between devices, per_device(): packed = lax.all_gather(packed, 'batch', axis=1, tiled=False)  51.7 us
    dot_general x1, matrix products, per_device(): jnp.einsum('etr,erh->eth', columns, second_all, preferred_element_type=jn...  36.6 us
    ppermute x1, waiting for transfers between devices, per_device(): total_own = total_own + lax.ppermute(total_sent, 'task', ring)  18 us
  transfers between devices with their start and end apart: 4, of which 3 were waited for; matrix products, arithmetic and copies ran while one was open for 3% of the time, Pallas kernels for 0%

commit v1 on v0

--- a/solution.py
+++ b/solution.py
@@ -10,7 +10,7 @@
     local_experts = w_first.shape[0]
     all_tasks = gate_weight.shape[2]
     own_tasks = tower_hidden.shape[0]
-    gathered = lax.all_gather(w_first, "batch", axis=1, tiled=True)
+    gathered = jnp.concatenate(lax.all_gather(w_first, "batch"), axis=1)
     deep_rows, deep_width = (w_second.shape[1], w_second.shape[2])
     last_rows, last_width = (w_third.shape[1], w_third.shape[2])
     halves = deep_width // last_width

time: 291 us -> 306 us (1.052)
  local copies, waits for them, and re-layouts: 10.6 us -> 29.6 us
  other arithmetic: 7.28 us -> 4.08 us
    reshape x0 -> x1, local copies, waits for them, and re-layouts: none -> 18.9 us  [per_device(): gathered = jnp.concatenate(lax.all_gather(w_first, 'batch'), axis=1)]
    convert_element_type x1 -> x0, other arithmetic: 3.22 us -> none  [per_device(): mix = (numer_own / total_own[:, :, None]).astype(jnp.bfloat16)]
where the time goes in v1:
time: 306 us
  waiting for transfers between devices  209 us (68%)
  matrix products  47.2 us (15%)
  local copies, waits for them, and re-layouts  29.6 us (10%)
  between operations  13.5 us (4%)
  other arithmetic  4.08 us (1%)
    all_gather x1, waiting for transfers between devices, per_device(): gathered = jnp.concatenate(lax.all_gather(w_first, 'batch'), axis=1)  140 us
    all_gather x1, waiting for transfers between devices, per_device(): packed = lax.all_gather(packed, 'batch', axis=1, tiled=False)  50.4 us
    dot_general x1, matrix products, per_device(): jnp.einsum('etr,erh->eth', columns, second_all, preferred_element_type=jn...  36.6 us
    reshape x1, local copies, waits for them, and re-layouts, per_device(): gathered = jnp.concatenate(lax.all_gather(w_first, 'batch'), axis=1)  18.9 us
    ppermute x1, waiting for transfers between devices, per_device(): total_own = total_own + lax.ppermute(total_sent, 'task', ring)  18 us
  transfers between devices with their start and end apart: 4, of which 3 were waited for; matrix products, arithmetic and copies ran while one was open for 3% of the time, Pallas kernels for 0%

profile of v1, /device:TPU:0, one launch (start us, length us, event | category | flops | bytes accessed | tf_op | source)
XLA Modules:
  0.0 305.9 jit_solution(2440761249411336292)
XLA Ops:
  6.5 0.7 all-gather.5.cloned.1.call-update
  7.3 0.0 all-gather.7.cloned.1.call-start
  7.3 1.0 fusion.30
  8.3 1.6 pad_maximum_fusion.1
  9.9 140.2 %all-gather.5.cloned.1.call-done = bf16[64,208,1024]{2,1,0:T(8,128)(2,1)} async-done(((bf16[4,208,1024]{2,1,0:T(8,128)(2,1)}), bf16[64,208,1024]{2,1,0:T(8,128)(2,1)}) %all-gather.5.cloned.1.call-update) | async-done | bytes 27262992 | tf_op jit(solution)/shard_map/all_gather | solution.py:13
  150.1 18.9 %copy.23 = bf16[4,16,208,1024]{3,2,1,0:T(8,128)(2,1)} copy(bf16[4,16,208,1024]{3,2,0,1:T(8,128)(2,1)} %bitcast.40) | data formatting | bytes 54525952 | tf_op jit(solution)/shard_map/reshape | solution.py:13
  169.0 0.0 all-gather.7.cloned.1.call-update
  169.2 4.1 %fusion.31 = (f32[768,4]{0,1:T(4,128)S(1)}, bf16[768,4,4]{0,2,1:T(4,128)(2,1)S(1)}) fusion(bf16[4,4,3328]{2,1,0:T(4,128)(2,1)S(1)} %dot_general.26, bf16[768,3328]{1,0:T(8,128)(2,1)} %param.7), kind=kOutput, calls=%fused_computation.36 | convolution fusion | flops 81810432 | bytes 5255168 | tf_op jit(solution)/shard_map/dot_general | solution.py:29
  173.2 1.3 copy.26
  174.5 50.4 %all-gather.7.cloned.1.call-done = bf16[4,2560,256]{2,1,0:T(8,128)(2,1)} async-done(((bf16[4,160,256]{2,1,0:T(8,128)(2,1)}), bf16[4,2560,256]{2,1,0:T(8,128)(2,1)}) %all-gather.7.cloned.1.call-update) | async-done | bytes 5242896 | tf_op jit(solution)/shard_map/all_gather | solution.py:22
  225.0 1.3 slice.22
  226.3 2.8 fusion.29
  229.1 2.5 pad_maximum_fusion
  231.5 36.6 %fusion = bf16[4,768,512]{2,1,0:T(8,128)(2,1)} fusion(bf16[4,1024,512]{2,1,0:T(8,128)(2,1)} %bitcast.43, bf16[4,3328,1024]{2,1,0:T(8,128)(2,1)} %bitcast.39, bf16[768,3328]{1,0:T(8,128)(2,1)} %param.7), kind=kOutput, calls=%fused_computation.1 | convolution fusion | flops 24165482496 | bytes 39714816 | tf_op jit(solution)/shard_map/etr,erh->eth/dot_general | solution.py:38
  268.1 2.9 maximum_convert_fusion.4
  271.1 1.5 fusion.14
  272.6 0.7 constant_dynamic-slice_fusion.1
  273.3 1.0 copy.49
  274.3 1.5 collective-permute-start
  275.8 0.6 collective-permute-start.1
  276.3 18.0 %collective-permute-done.1 = f32[768,2]{0,1:T(2,128)S(1)} collective-permute-done((f32[768,2]{0,1:T(2,128)S(1)}, f32[768,2]{0,1:T(2,128)S(1)}, u32[]{:S(2)}, u32[]{:S(2)}) %collective-permute-start.1) | collective-permute-done | bytes 6176 | tf_op jit(solution)/shard_map/ppermute | solution.py:55
  294.4 1.8 constant_dynamic-slice_fusion.2
  296.3 2.2 fusion.18
  298.4 0.6 copy.50
  (14 shorter events, 0.1 us)
Async XLA Ops:
  6.5 289.7 %copy-start = (bf16[2,256,128]{2,1,0:T(8,128)(2,1)S(1)}, bf16[2,256,128]{2,1,0:T(8,128)(2,1)}, u32[]{:S(2)}) copy-start(bf16[2,256,128]{2,1,0:T(8,128)(2,1)} %param.12) | copy-start | bytes 393220
  6.5 143.6 %all-gather.5.cloned.1.call-start = ((), (), s32[]{:S(2)}) async-start(), calls=%async_computation | async-start | bytes 28966912 | tf_op jit(solution)/shard_map/all_gather | solution.py:13
  7.3 217.7 %all-gather.7.cloned.1.call-start = ((), (), s32[]{:S(2)}) async-start(), calls=%async_computation.1 | async-start | bytes 5570560 | tf_op jit(solution)/shard_map/all_gather | solution.py:22
  150.1 19.0 %copy-start.2 = (bf16[3328,4,4]{0,2,1:T(4,128)(2,1)S(1)}, bf16[3328,4,4]{0,2,1:T(4,128)(2,1)}, u32[]{:S(2)}) copy-start(bf16[3328,4,4]{0,2,1:T(4,128)(2,1)} %param.8) | copy-start | bytes 319492
  268.1 3.0 copy-start.1
  272.6 23.7 %copy-start.3 = (bf16[2,128]{1,0:T(2,128)(2,1)S(1)}, bf16[2,128]{1,0:T(2,128)(2,1)}, u32[]{:S(2)}) copy-start(bf16[2,128]{1,0:T(2,128)(2,1)} %param.13) | copy-start | bytes 1540
  274.3 21.9 %collective-permute-start = (bf16[768,2,256]{2,0,1:T(8,128)(2,1)}, bf16[768,2,256]{2,0,1:T(8,128)(2,1)}, u32[]{:S(2)}, u32[]{:S(2)}) collective-permute-start(bf16[768,2,256]{2,0,1:T(8,128)(2,1)} %copy.49), channel_id=1, source_target_pairs={{0,16},{16,0},{1,17},{17,1},{2,18},{18,2},{3,19},{19,3},{4,20},{20... | collective-permute-start | bytes 2359304 | tf_op jit(solution)/shard_map/ppermute | solution.py:54
  275.8 18.6 %collective-permute-start.1 = (f32[768,2]{0,1:T(2,128)S(1)}, f32[768,2]{0,1:T(2,128)S(1)}, u32[]{:S(2)}, u32[]{:S(2)}) collective-permute-start(f32[768,2]{0,1:T(2,128)S(1)} %constant_dynamic-slice_fusion), channel_id=1, source_target_pairs={{0,16},{16,0},{1,17},{17,1},{2,18},{18,2},{3,19},{19,3},{4,20},{20... | collective-permute-start | bytes 18440 | tf_op jit(solution)/shard_map/ppermute | solution.py:55
Sparse Core Ops, SparseCore 0:
  8.9 141.1 all-gather.4
  169.2 55.7 all-gather.6
